TPU v7x, 128 devices: a whole 4x4x4 slice. The times are simulated.
128 devices in a mesh: gx: 16 (over y, x), gy: 8 (over z, core).
Axes of the slice: x: 4, y: 4, z: 4, core: 2. Of those that a mesh axis runs over, the one named last changes fastest.
Arguments:
- basis: float32 [32, 256, 128, 256], P(None, 'gx', 'gy'), may hold values from -0.09375 to 0.09375
- reaction: float32 [256, 128, 256], P('gx', 'gy'), may hold values from 0.5 to 4
Outputs:
- extended: float32 [32, 256, 128, 256], P(None, 'gx', 'gy')
- coarse: float32 [128, 5, 32, 32], replicated
All inputs are finite; a program needn't handle non-finite values.
Results may differ from a plain program's by a relative error of at most 0.000071.
Values sent between devices are 32-bit elements; how exact they have to be, the bound alone decides.
No kernel may reach another device: no remote copies, remote signals or barrier semaphores. Data moves between devices by JAX's collectives and lax.ppermute only.
A program may use at most 128 MiB of HBM per device.

v0:
```python
import jax
import jax.numpy as jnp
from jax import lax
from jax.sharding import PartitionSpec as P

SWEEPS = 4
OMEGA = 0.8


def with_halo(shard, sides, width):
    edges = {}
    for axis, dim in sides:
        size, length = (lax.axis_size(axis), shard.shape[dim])
        up = [(i, (i + 1) % size) for i in range(size - 1)]
        last = lax.slice_in_dim(shard, length - width, length, axis=dim)
        first = lax.slice_in_dim(shard, 0, width, axis=dim)
        edges[dim] = (
            lax.ppermute(last, axis, up),
            lax.ppermute(first, axis, [(b, a) for a, b in up]),
        )
    done = []
    for _, dim in sides:
        low, high = edges[dim]
        around = [(width, width) if d in done else (0, 0) for d in range(shard.ndim)]
        shard = jnp.concatenate([jnp.pad(low, around), shard, jnp.pad(high, around)], axis=dim)
        done.append(dim)
    return shard


def stencil(field, coef):
    padded = jnp.pad(field, ((0, 0), (1, 1), (1, 1), (1, 1)))
    beside = padded[:, 2:, 1:-1, 1:-1] + padded[:, :-2, 1:-1, 1:-1]
    beside = beside + padded[:, 1:-1, 2:, 1:-1] + padded[:, 1:-1, :-2, 1:-1]
    beside = beside + padded[:, 1:-1, 1:-1, 2:] + padded[:, 1:-1, 1:-1, :-2]
    return (6.0 + coef) * field - beside


def couple(own, other):
    width = own.shape[0]
    return -jnp.dot(
        own.reshape(width, -1),
        other.reshape(width, -1).T,
        precision=lax.Precision.HIGHEST,
        preferred_element_type=jnp.float32,
    )


def on_device(basis, reaction):
    width, cx, cy, cz = basis.shape
    padded = with_halo(basis, (("gx", 1), ("gy", 2)), 1)
    left_face = padded[:, 0, 1:-1, :]
    right_face = padded[:, -1, 1:-1, :]
    lower_face = padded[:, 1:-1, 0, :]
    upper_face = padded[:, 1:-1, -1, :]
    xpos = lax.broadcasted_iota(jnp.int32, (cx, cy, cz), 0)
    ypos = lax.broadcasted_iota(jnp.int32, (cx, cy, cz), 1)
    inner = (xpos >= 1) & (xpos <= cx - 2) & (ypos >= 1) & (ypos <= cy - 2)
    phi = basis
    for sweep in range(SWEEPS):
        update = OMEGA * stencil(phi, reaction) / (6.0 + reaction)
        phi = phi - jnp.where(inner[None], update, jnp.float32(0.0))
    applied = stencil(phi, reaction)
    diag = jnp.dot(
        phi.reshape(width, -1),
        applied.reshape(width, -1).T,
        precision=lax.Precision.HIGHEST,
        preferred_element_type=jnp.float32,
    )
    blocks = jnp.stack(
        [
            diag,
            couple(basis[:, 0], left_face),
            couple(basis[:, -1], right_face),
            couple(basis[:, :, 0], lower_face),
            couple(basis[:, :, -1], upper_face),
        ]
    )
    coarse = lax.all_gather(blocks[None], ("gx", "gy"), axis=0, tiled=True)
    return (phi, coarse)


def solution(mesh):
    placed = (P(None, "gx", "gy", None), P("gx", "gy", None))
    return jax.shard_map(
        on_device,
        mesh=mesh,
        in_specs=placed,
        out_specs=(P(None, "gx", "gy", None), P()),
        check_vma=False,
    )
```

profile of v0, /device:TPU:1, one launch (start us, length us, event | category | flops | bytes accessed | tf_op | source)
XLA Modules:
  0.0 217.7 jit_solution(16846393999798236059)
XLA Ops:
  7.2 1.4 fusion.77
  8.7 1.1 copy.20
  9.8 4.9 %collective-permute-start = (f32[32,1,16,256]{3,0,2,1:T(8,128)}, f32[32,1,16,256]{3,0,2,1:T(8,128)}, u32[]{:S(2)}, u32[]{:S(2)}) collective-permute-start(f32[32,1,16,256]{3,0,2,1:T(8,128)} %copy.20), channel_id=1, source_target_pairs={{0,8},{8,16},{16,24},{24,32},{32,40},{40,48},{48,56},{56,64},{64,7... | collective-permute-start | bytes 1572872 | tf_op jit(solution)/shard_map/ppermute | solution.py:18
  14.6 1.1 copy.19
  15.8 1.3 collective-permute-start.1
  17.1 4.4 %fusion.76 = (f32[32,16,1,256]{3,2,1,0:T(1,128)S(1)}, f32[32,16,1,256]{3,2,1,0:T(1,128)S(1)}) fusion(f32[32,16,16,256]{3,2,1,0:T(8,128)} %param.2), kind=kLoop, calls=%fused_computation.110 | loop fusion | bytes 2097152 | tf_op jit(solution)/shard_map/slice | solution.py:74
  21.5 1.1 copy.22
  22.6 4.4 %collective-permute-start.2 = (f32[32,16,1,256]{3,0,1,2:T(8,128)}, f32[32,16,1,256]{3,0,1,2:T(8,128)}, u32[]{:S(2)}, u32[]{:S(2)}) collective-permute-start(f32[32,16,1,256]{3,0,1,2:T(8,128)} %copy.22), channel_id=1, source_target_pairs={{0,1},{1,2},{2,3},{3,4},{4,5},{5,6},{6,7},{8,9},{9,10},{10,11},{11... | collective-permute-start | bytes 1572872 | tf_op jit(solution)/shard_map/ppermute | solution.py:18
  27.0 1.1 copy.21
  28.1 2.1 collective-permute-start.3
  30.2 1.0 broadcast_add_fusion
  31.3 9.6 %select_subtract_fusion.3 = f32[32,16,16,256]{3,2,1,0:T(8,128)} fusion(f32[32,16,16,256]{3,2,1,0:T(8,128)S(1)} %copy-done.1, f32[16,16,256]{2,1,0:T(8,128)S(1)} %broadcast_add_fusion, pred[16,16,256]{2,1,0:T(8,128)(4,1)S(1)} %and_and_fusion), kind=kLoop, calls=%fused_computation.74 | loop fusion | flops 23068672 | bytes 17104896 | tf_op jit(solution)/shard_map/sub | solution.py:61
  40.9 21.9 %select_subtract_fusion.2 = f32[32,16,16,256]{3,2,1,0:T(8,128)S(1)} fusion(f32[32,16,16,256]{3,2,1,0:T(8,128)} %select_subtract_fusion.3, f32[16,16,256]{2,1,0:T(8,128)S(1)} %broadcast_add_fusion, pred[16,16,256]{2,1,0:T(8,128)(4,1)S(1)} %and_and_fusion), kind=kLoop, calls=%fused_computation.73 | loop fusion | flops 23068672 | bytes 17104896 | tf_op jit(solution)/shard_map/sub | solution.py:61
  62.8 9.6 %select_subtract_fusion.1 = f32[32,16,16,256]{3,2,1,0:T(8,128)} fusion(f32[32,16,16,256]{3,2,1,0:T(8,128)S(1)} %select_subtract_fusion.2, f32[16,16,256]{2,1,0:T(8,128)S(1)} %broadcast_add_fusion, pred[16,16,256]{2,1,0:T(8,128)(4,1)S(1)} %and_and_fusion), kind=kLoop, calls=%fused_computation.72 | loop fusion | flops 23068672 | bytes 17104896 | tf_op jit(solution)/shard_map/sub | solution.py:61
  72.4 21.9 %select_subtract_fusion = f32[32,16,16,256]{3,2,1,0:T(8,128)S(1)} fusion(f32[32,16,16,256]{3,2,1,0:T(8,128)} %select_subtract_fusion.1, f32[16,16,256]{2,1,0:T(8,128)S(1)} %broadcast_add_fusion, pred[16,16,256]{2,1,0:T(8,128)(4,1)S(1)} %and_and_fusion), kind=kLoop, calls=%fused_computation.71 | loop fusion | flops 23068672 | bytes 17104896 | tf_op jit(solution)/shard_map/sub | solution.py:61
  94.3 9.3 %fusion.37 = f32[32,16,16,256]{3,2,1,0:T(8,128)} fusion(f32[32,16,16,256]{3,2,1,0:T(8,128)S(1)} %select_subtract_fusion, f32[16,16,256]{2,1,0:T(8,128)S(1)} %broadcast_add_fusion), kind=kLoop, calls=%fused_computation.67 | loop fusion | flops 14680064 | bytes 17039360 | tf_op jit(solution)/shard_map/sub | solution.py:35
  103.6 16.2 %fusion.58 = f32[5,32,32]{2,1,0:T(8,128)S(1)} fusion(f32[32,16,16,256]{3,2,1,0:T(8,128)} %fusion.37, f32[32,16,16,256]{3,2,1,0:T(8,128)S(1)} %select_subtract_fusion), kind=kOutput, calls=%fused_computation.92 | convolution fusion | flops 805306368 | bytes 16793600 | tf_op jit(solution)/shard_map/dot_general | solution.py:63
  119.8 1.9 fusion.52
  121.7 1.9 fusion.49
  123.6 1.9 fusion.46
  125.5 0.8 fusion.43
  126.3 0.6 copy-done.2
  127.0 74.6 %all-gather.3.cloned.1.call-done = f32[640,32,32]{2,1,0:T(8,128)} async-done(((f32[5,32,32]{2,1,0:T(8,128)}), f32[640,32,32]{2,1,0:T(8,128)}) %all-gather.3.cloned.1.call-update) | async-done | bytes 2621456 | tf_op jit(solution)/shard_map/all_gather | solution.py:78
  201.6 9.2 %copy.17 = f32[128,5,32,32]{0,3,2,1:T(8,128)} copy(f32[128,5,32,32]{3,2,1,0:T(8,128)} %bitcast.81) | data formatting | bytes 5242880
  (14 shorter events, 0.2 us)
Async XLA Ops:
  7.2 194.4 %all-gather.3.cloned.1.call-start = ((), (), s32[]{:S(2)}) async-start(), calls=%async_computation | async-start | bytes 10567680 | tf_op jit(solution)/shard_map/all_gather | solution.py:78
  7.2 24.1 %copy-start.1 = (f32[32,16,16,256]{3,2,1,0:T(8,128)S(1)}, f32[32,16,16,256]{3,2,1,0:T(8,128)}, u32[]{:S(2)}) copy-start(f32[32,16,16,256]{3,2,1,0:T(8,128)} %param.2) | copy-start | bytes 25165828
  9.8 110.1 %collective-permute-start = (f32[32,1,16,256]{3,0,2,1:T(8,128)}, f32[32,1,16,256]{3,0,2,1:T(8,128)}, u32[]{:S(2)}, u32[]{:S(2)}) collective-permute-start(f32[32,1,16,256]{3,0,2,1:T(8,128)} %copy.20), channel_id=1, source_target_pairs={{0,8},{8,16},{16,24},{24,32},{32,40},{40,48},{48,56},{56,64},{64,7... | collective-permute-start | bytes 1572872 | tf_op jit(solution)/shard_map/ppermute | solution.py:18
  15.8 105.9 %collective-permute-start.1 = (f32[32,1,16,256]{3,0,2,1:T(8,128)}, f32[32,1,16,256]{3,0,2,1:T(8,128)}, u32[]{:S(2)}, u32[]{:S(2)}) collective-permute-start(f32[32,1,16,256]{3,0,2,1:T(8,128)} %copy.19), channel_id=1, source_target_pairs={{8,0},{16,8},{24,16},{32,24},{40,32},{48,40},{56,48},{64,56},{72,6... | collective-permute-start | bytes 1572872 | tf_op jit(solution)/shard_map/ppermute | solution.py:19
  22.6 101.0 %collective-permute-start.2 = (f32[32,16,1,256]{3,0,1,2:T(8,128)}, f32[32,16,1,256]{3,0,1,2:T(8,128)}, u32[]{:S(2)}, u32[]{:S(2)}) collective-permute-start(f32[32,16,1,256]{3,0,1,2:T(8,128)} %copy.22), channel_id=1, source_target_pairs={{0,1},{1,2},{2,3},{3,4},{4,5},{5,6},{6,7},{8,9},{9,10},{10,11},{11... | collective-permute-start | bytes 1572872 | tf_op jit(solution)/shard_map/ppermute | solution.py:18
  28.1 97.4 %collective-permute-start.3 = (f32[32,16,1,256]{3,0,1,2:T(8,128)}, f32[32,16,1,256]{3,0,1,2:T(8,128)S(1)}, u32[]{:S(2)}, u32[]{:S(2)}) collective-permute-start(f32[32,16,1,256]{3,0,1,2:T(8,128)} %copy.21), channel_id=1, source_target_pairs={{1,0},{2,1},{3,2},{4,3},{5,4},{6,5},{7,6},{9,8},{10,9},{11,10},{12... | collective-permute-start | bytes 1572872 | tf_op jit(solution)/shard_map/ppermute | solution.py:19
  94.3 9.3 %copy-start = (f32[32,16,16,256]{3,2,1,0:T(8,128)}, f32[32,16,16,256]{3,2,1,0:T(8,128)S(1)}, u32[]{:S(2)}) copy-start(f32[32,16,16,256]{3,2,1,0:T(8,128)S(1)} %select_subtract_fusion) | copy-start | bytes 25165828
  126.3 0.6 copy-start.2
Sparse Core Ops, SparseCore 0:
  127.1 74.4 all-gather.2
where the time goes:
time: 218 us
  waiting for transfers between devices  74.6 us (34%)
  other arithmetic  73.3 us (34%)
  matrix products  22.7 us (10%)
  local copies, waits for them, and re-layouts  20.2 us (9%)
  between operations  14.2 us (7%)
  starting transfers between devices  12.7 us (6%)
    all_gather x1, waiting for transfers between devices, on_device(): coarse = lax.all_gather(blocks[None], ('gx', 'gy'), axis=0, tiled=True)  74.6 us
    sub x4, other arithmetic, on_device(): phi = phi - jnp.where(inner[None], update, jnp.float32(0.0))  63 us
    dot_general x1, matrix products, on_device(): jnp.dot(phi.reshape(width, -1), applied.reshape(width, -1).T, precision=l...  16.2 us
    unnamed x11, local copies, waits for them, and re-layouts  14.3 us
    sub x1, other arithmetic, stencil(): return (6.0 + coef) * field - beside  9.28 us
    ppermute x2, starting transfers between devices, with_halo(): lax.ppermute(last, axis, up)  9.26 us
    dot_general x4, matrix products, couple(): jnp.dot(own.reshape(width, -1), other.reshape(width, -1).T, precision=lax...  6.45 us
    slice x1, local copies, waits for them, and re-layouts, on_device(): basis[:, :, 0]  4.41 us
  transfers between devices with their start and end apart: 5, of which 1 were waited for; matrix products, arithmetic and copies ran while one was open for 47% of the time, Pallas kernels for 0%

commit v1 on v0

--- a/solution.py
+++ b/solution.py
@@ -75,7 +75,9 @@
             couple(basis[:, :, -1], upper_face),
         ]
     )
-    coarse = lax.all_gather(blocks[None], ("gx", "gy"), axis=0, tiled=True)
+    part = blocks[None]
+    sent = jnp.stack([part] * lax.axis_size(("gx", "gy")))
+    coarse = jnp.concatenate(lax.all_to_all(sent, ("gx", "gy"), 0, 0), axis=0)
     return (phi, coarse)
 
 

time: 218 us -> 208 us (0.954)
  waiting for transfers between devices: 74.6 us -> 0.01 us
  blocking collectives: 0 us -> 46.5 us
  local copies, waits for them, and re-layouts: 20.2 us -> 42.1 us
  between operations: 14.2 us -> 0.81 us
  other arithmetic: 73.3 us -> 82.4 us
    all_gather x1 -> x0, waiting for transfers between devices: 74.6 us -> none  [on_device(): coarse = lax.all_gather(blocks[None], ('gx', 'gy'), axis=0, tiled=True)]
    all_to_all x0 -> x1, blocking collectives: none -> 46.5 us  [on_device(): coarse = jnp.concatenate(lax.all_to_all(sent, ('gx', 'gy'), 0, 0), axis=0)]
    unnamed x11, local copies, waits for them, and re-layouts: 14.3 us -> 30.3 us
    all_to_all x0 -> x1, other arithmetic: none -> 9.11 us  [on_device(): coarse = jnp.concatenate(lax.all_to_all(sent, ('gx', 'gy'), 0, 0), axis=0)]
    another operation x0 -> x1, local copies, waits for them, and re-layouts: none -> 5.31 us  [on_device(): sent = jnp.stack([part] * lax.axis_size(('gx', 'gy')))]
  transfers between devices with their start and end apart: 5 -> 4, of which waited for: 1 -> 0; matrix products, arithmetic and copies ran while one was open for 47% -> 50% of each run, Pallas kernels for 0% -> 0%
where the time goes in v1:
time: 208 us; the launch traced here: 207 us
  other arithmetic  82.4 us (40%)
  blocking collectives  46.5 us (22%)
  local copies, waits for them, and re-layouts  42.1 us (20%)
  matrix products  22.7 us (11%)
  starting transfers between devices  12.6 us (6%)
    sub x4, other arithmetic, on_device(): phi = phi - jnp.where(inner[None], update, jnp.float32(0.0))  63 us
    all_to_all x1, blocking collectives, on_device(): coarse = jnp.concatenate(lax.all_to_all(sent, ('gx', 'gy'), 0, 0), axis=0)  46.5 us
    unnamed x11, local copies, waits for them, and re-layouts  30.3 us
    dot_general x1, matrix products, on_device(): jnp.dot(phi.reshape(width, -1), applied.reshape(width, -1).T, precision=l...  16.2 us
    ppermute x2, starting transfers between devices, with_halo(): lax.ppermute(last, axis, up)  9.27 us
    sub x1, other arithmetic, stencil(): return (6.0 + coef) * field - beside  9.2 us
    all_to_all x1, other arithmetic, on_device(): coarse = jnp.concatenate(lax.all_to_all(sent, ('gx', 'gy'), 0, 0), axis=0)  9.11 us
    dot_general x4, matrix products, couple(): jnp.dot(own.reshape(width, -1), other.reshape(width, -1).T, precision=lax...  6.45 us
  transfers between devices with their start and end apart: 4, of which 0 were waited for; matrix products, arithmetic and copies ran while one was open for 50% of the time, Pallas kernels for 0%

profile of v1, /device:TPU:1, one launch (start us, length us, event | category | flops | bytes accessed | tf_op | source)
XLA Modules:
  0.0 207.1 jit_solution(14396473811292391515)
XLA Ops:
  0.6 1.4 fusion.77
  2.1 1.1 copy.19
  3.2 4.9 %collective-permute-start = (f32[32,1,16,256]{3,0,2,1:T(8,128)}, f32[32,1,16,256]{3,0,2,1:T(8,128)}, u32[]{:S(2)}, u32[]{:S(2)}) collective-permute-start(f32[32,1,16,256]{3,0,2,1:T(8,128)} %copy.19), channel_id=1, source_target_pairs={{0,8},{8,16},{16,24},{24,32},{32,40},{40,48},{48,56},{56,64},{64,7... | collective-permute-start | bytes 1572872 | tf_op jit(solution)/shard_map/ppermute | solution.py:18
  8.1 1.1 copy.18
  9.2 1.3 collective-permute-start.1
  10.5 4.4 %fusion.76 = (f32[32,16,1,256]{3,2,1,0:T(1,128)S(1)}, f32[32,16,1,256]{3,2,1,0:T(1,128)S(1)}) fusion(f32[32,16,16,256]{3,2,1,0:T(8,128)} %param.2), kind=kLoop, calls=%fused_computation.110 | loop fusion | bytes 2097152 | tf_op jit(solution)/shard_map/slice | solution.py:74
  16.0 4.4 %collective-permute-start.2 = (f32[32,16,1,256]{3,0,1,2:T(8,128)}, f32[32,16,1,256]{3,0,1,2:T(8,128)}, u32[]{:S(2)}, u32[]{:S(2)}) collective-permute-start(f32[32,16,1,256]{3,0,1,2:T(8,128)} %copy.21), channel_id=1, source_target_pairs={{0,1},{1,2},{2,3},{3,4},{4,5},{5,6},{6,7},{8,9},{9,10},{10,11},{11... | collective-permute-start | bytes 1572872 | tf_op jit(solution)/shard_map/ppermute | solution.py:18
  20.4 1.1 copy.20
  21.5 2.1 %collective-permute-start.3 = (f32[32,16,1,256]{3,0,1,2:T(8,128)}, f32[32,16,1,256]{3,0,1,2:T(8,128)S(1)}, u32[]{:S(2)}, u32[]{:S(2)}) collective-permute-start(f32[32,16,1,256]{3,0,1,2:T(8,128)} %copy.20), channel_id=1, source_target_pairs={{1,0},{2,1},{3,2},{4,3},{5,4},{6,5},{7,6},{9,8},{10,9},{11,10},{12... | collective-permute-start | bytes 1572872 | tf_op jit(solution)/shard_map/ppermute | solution.py:19
  24.7 9.6 %select_subtract_fusion.3 = f32[32,16,16,256]{3,2,1,0:T(8,128)} fusion(f32[32,16,16,256]{3,2,1,0:T(8,128)S(1)} %copy-done.1, f32[16,16,256]{2,1,0:T(8,128)S(1)} %broadcast_add_fusion, pred[16,16,256]{2,1,0:T(8,128)(4,1)S(1)} %and_and_fusion), kind=kLoop, calls=%fused_computation.74 | loop fusion | flops 23068672 | bytes 17104896 | tf_op jit(solution)/shard_map/sub | solution.py:61
  34.3 21.9 %select_subtract_fusion.2 = f32[32,16,16,256]{3,2,1,0:T(8,128)S(1)} fusion(f32[32,16,16,256]{3,2,1,0:T(8,128)} %select_subtract_fusion.3, f32[16,16,256]{2,1,0:T(8,128)S(1)} %broadcast_add_fusion, pred[16,16,256]{2,1,0:T(8,128)(4,1)S(1)} %and_and_fusion), kind=kLoop, calls=%fused_computation.73 | loop fusion | flops 23068672 | bytes 17104896 | tf_op jit(solution)/shard_map/sub | solution.py:61
  56.2 9.6 %select_subtract_fusion.1 = f32[32,16,16,256]{3,2,1,0:T(8,128)} fusion(f32[32,16,16,256]{3,2,1,0:T(8,128)S(1)} %select_subtract_fusion.2, f32[16,16,256]{2,1,0:T(8,128)S(1)} %broadcast_add_fusion, pred[16,16,256]{2,1,0:T(8,128)(4,1)S(1)} %and_and_fusion), kind=kLoop, calls=%fused_computation.72 | loop fusion | flops 23068672 | bytes 17104896 | tf_op jit(solution)/shard_map/sub | solution.py:61
  65.8 21.9 %select_subtract_fusion = f32[32,16,16,256]{3,2,1,0:T(8,128)S(1)} fusion(f32[32,16,16,256]{3,2,1,0:T(8,128)} %select_subtract_fusion.1, f32[16,16,256]{2,1,0:T(8,128)S(1)} %broadcast_add_fusion, pred[16,16,256]{2,1,0:T(8,128)(4,1)S(1)} %and_and_fusion), kind=kLoop, calls=%fused_computation.71 | loop fusion | flops 23068672 | bytes 17104896 | tf_op jit(solution)/shard_map/sub | solution.py:61
  87.7 9.2 %fusion.37 = f32[32,16,16,256]{3,2,1,0:T(8,128)} fusion(f32[32,16,16,256]{3,2,1,0:T(8,128)S(1)} %select_subtract_fusion, f32[16,16,256]{2,1,0:T(8,128)S(1)} %broadcast_add_fusion), kind=kLoop, calls=%fused_computation.67 | loop fusion | flops 14680064 | bytes 17039360 | tf_op jit(solution)/shard_map/sub | solution.py:35
  96.9 16.2 %fusion.58 = f32[5,32,32]{2,1,0:T(8,128)S(1)} fusion(f32[32,16,16,256]{3,2,1,0:T(8,128)} %fusion.37, f32[32,16,16,256]{3,2,1,0:T(8,128)S(1)} %select_subtract_fusion), kind=kOutput, calls=%fused_computation.92 | convolution fusion | flops 805306368 | bytes 16793600 | tf_op jit(solution)/shard_map/dot_general | solution.py:63
  113.2 1.9 fusion.52
  115.1 1.9 fusion.49
  117.0 1.9 fusion.46
  119.7 5.3 %stack.27 = f32[128,1,5,32,32]{4,3,2,1,0:T(8,128)} broadcast(f32[5,32,32]{2,1,0:T(8,128)S(1)} %fusion.43), dimensions={2,3,4} | broadcast | bytes 2641920 | tf_op jit(solution)/shard_map/stack | solution.py:79
  125.0 9.3 %reshape.52 = f32[128,1,5120]{2,1,0:T(1,128)} reshape(f32[128,1,5,32,32]{4,3,2,1,0:T(8,128)} %stack.27) | data formatting | bytes 5242880
  134.2 46.5 %all_to_all.5 = f32[128,1,5120]{2,1,0:T(1,128)S(1)} all-to-all(f32[128,1,5120]{2,1,0:T(1,128)} %reshape.52), channel_id=1, replica_groups=mesh['gx'=16,'gy'=8] {'gx','gy'}, dimensions={0} | all-to-all | bytes 5242880 | tf_op jit(solution)/shard_map/all_to_all | solution.py:80
  181.4 9.1 %reduce = f32[128,5120]{1,0:T(8,128)} reduce(f32[128,1,5120]{2,1,0:T(1,128)S(1)} %all_to_all.5, f32[]{:T(128)} %broadcast.62), dimensions={1}, to_apply=%all_to_all.3.reduce_sub_computation | reduce | bytes 5242884 | tf_op jit(solution)/shard_map/all_to_all | solution.py:80
  190.5 7.4 %reshape.53 = f32[128,1,5,32,32]{4,3,2,1,0:T(8,128)} reshape(f32[128,5120]{1,0:T(8,128)} %reduce) | data formatting | bytes 5242880
  197.8 9.2 %copy.16 = f32[128,5,32,32]{0,3,2,1:T(8,128)} copy(f32[128,5,32,32]{3,2,1,0:T(8,128)} %bitcast.81) | data formatting | bytes 5242880
  (15 shorter events, 3.6 us)
Async XLA Ops:
  0.6 24.1 %copy-start.1 = (f32[32,16,16,256]{3,2,1,0:T(8,128)S(1)}, f32[32,16,16,256]{3,2,1,0:T(8,128)}, u32[]{:S(2)}) copy-start(f32[32,16,16,256]{3,2,1,0:T(8,128)} %param.2) | copy-start | bytes 25165828
  3.2 110.0 %collective-permute-start = (f32[32,1,16,256]{3,0,2,1:T(8,128)}, f32[32,1,16,256]{3,0,2,1:T(8,128)}, u32[]{:S(2)}, u32[]{:S(2)}) collective-permute-start(f32[32,1,16,256]{3,0,2,1:T(8,128)} %copy.19), channel_id=1, source_target_pairs={{0,8},{8,16},{16,24},{24,32},{32,40},{40,48},{48,56},{56,64},{64,7... | collective-permute-start | bytes 1572872 | tf_op jit(solution)/shard_map/ppermute | solution.py:18
  9.2 105.8 %collective-permute-start.1 = (f32[32,1,16,256]{3,0,2,1:T(8,128)}, f32[32,1,16,256]{3,0,2,1:T(8,128)}, u32[]{:S(2)}, u32[]{:S(2)}) collective-permute-start(f32[32,1,16,256]{3,0,2,1:T(8,128)} %copy.18), channel_id=1, source_target_pairs={{8,0},{16,8},{24,16},{32,24},{40,32},{48,40},{56,48},{64,56},{72,6... | collective-permute-start | bytes 1572872 | tf_op jit(solution)/shard_map/ppermute | solution.py:19
  16.0 100.9 %collective-permute-start.2 = (f32[32,16,1,256]{3,0,1,2:T(8,128)}, f32[32,16,1,256]{3,0,1,2:T(8,128)}, u32[]{:S(2)}, u32[]{:S(2)}) collective-permute-start(f32[32,16,1,256]{3,0,1,2:T(8,128)} %copy.21), channel_id=1, source_target_pairs={{0,1},{1,2},{2,3},{3,4},{4,5},{5,6},{6,7},{8,9},{9,10},{10,11},{11... | collective-permute-start | bytes 1572872 | tf_op jit(solution)/shard_map/ppermute | solution.py:18
  21.5 97.3 %collective-permute-start.3 = (f32[32,16,1,256]{3,0,1,2:T(8,128)}, f32[32,16,1,256]{3,0,1,2:T(8,128)S(1)}, u32[]{:S(2)}, u32[]{:S(2)}) collective-permute-start(f32[32,16,1,256]{3,0,1,2:T(8,128)} %copy.20), channel_id=1, source_target_pairs={{1,0},{2,1},{3,2},{4,3},{5,4},{6,5},{7,6},{9,8},{10,9},{11,10},{12... | collective-permute-start | bytes 1572872 | tf_op jit(solution)/shard_map/ppermute | solution.py:19
  87.7 9.2 %copy-start = (f32[32,16,16,256]{3,2,1,0:T(8,128)}, f32[32,16,16,256]{3,2,1,0:T(8,128)S(1)}, u32[]{:S(2)}) copy-start(f32[32,16,16,256]{3,2,1,0:T(8,128)S(1)} %select_subtract_fusion) | copy-start | bytes 25165828
